TPU v7x, 32 devices: a whole 2x2x4 slice. The times are simulated.
32 devices in a mesh: row: 4 (over y, core), col: 8 (over z, x).
Axes of the slice: x: 2, y: 2, z: 4, core: 2. Of those that a mesh axis runs over, the one named last changes fastest.
Arguments:
- sources: bfloat16 [4, 8, 4, 256, 256], P('row', 'col'), may hold values from -6 to 6
- history: bfloat16 [4, 8, 8, 256, 256], P(None, 'col'), may hold values from -4 to 4
- inverse_diagonal: float32 [4, 8, 256], P('row', 'col'), may hold values from 0.3 to 0.6
- far_cores: bfloat16 [4, 8, 32, 4, 8, 8, 32], P('row', None, None, None, 'col'), may hold values from -0.09375 to 0.09375
- target_basis: bfloat16 [4, 8, 256, 32], P('row', 'col'), may hold values from -1 to 1
- source_basis: bfloat16 [4, 8, 256, 32], P(None, 'col'), may hold values from -0.375 to 0.375
- near_blocks: bfloat16 [4, 8, 3, 256, 8, 256], P('row', 'col'), may hold values from -0.078125 to 0.078125
- near_tile: int32 [4, 8, 3], P('row', 'col'), may hold values from 0 to 3
- near_count: int32 [4, 8], P('row', 'col'), may hold values from 1 to 3, as said below
Outputs:
- new_steps: bfloat16 [4, 8, 4, 256, 256], P('row', 'col')
- energies: float32 [4, 256], replicated
Inputs may be any that keep to these rules, and one draw needn't show every extreme that they name: Only slots below near_count are used; in every draw some tile has all 3 slots live.
All inputs are finite; a program needn't handle non-finite values.
Results may differ from a plain program's by a relative error of at most 0.011.
Values may be sent and summed in bfloat16 or wider, within the bound.
A program may use at most 192 MiB of HBM per device.

v0:
```python
import jax
import jax.numpy as jnp
from jax import lax
from jax.sharding import PartitionSpec as P


def local(
    sources,
    history,
    inverse_diagonal,
    far_cores,
    target_basis,
    source_basis,
    near_blocks,
    near_tile,
    near_count,
):
    row_count = history.shape[0]
    col_count = far_cores.shape[1]
    rank_size = far_cores.shape[2]
    lag_count = history.shape[2]
    tile_size = history.shape[3]
    field_count = history.shape[4]
    step_count = sources.shape[2]
    panel_total = row_count * col_count * tile_size
    column_past = history[:, 0]
    basis = source_basis[:, 0]
    projected = jnp.einsum(
        "pta,pktx->pkax", basis, column_past, preferred_element_type=jnp.float32
    ).astype(jnp.bfloat16)
    core_matrix = far_cores.reshape(col_count * rank_size, row_count * lag_count * rank_size)
    own_basis = target_basis[0, 0]
    scaling = inverse_diagonal[0, 0][:, None]
    blocks_here = near_blocks[0, 0]
    tiles_here = near_tile[0, 0]
    live_count = near_count[0, 0]
    outputs = []
    energy_rows = []
    for moment in range(step_count):
        partial_value = jnp.dot(
            core_matrix,
            projected.reshape(row_count * lag_count * rank_size, field_count),
            preferred_element_type=jnp.float32,
        )

        def add_block(slot, total):
            source = lax.dynamic_index_in_dim(
                column_past, tiles_here[slot], 0, keepdims=False
            ).reshape(lag_count * tile_size, field_count)
            block = lax.dynamic_index_in_dim(blocks_here, slot, 0, keepdims=False).reshape(
                tile_size, lag_count * tile_size
            )
            return total + jnp.dot(block, source, preferred_element_type=jnp.float32)

        near = lax.fori_loop(
            0, live_count, add_block, jnp.zeros((tile_size, field_count), jnp.float32)
        )
        own_core = lax.psum_scatter(
            partial_value.astype(jnp.bfloat16), "col", scatter_dimension=0, tiled=True
        )
        far = jnp.dot(own_basis, own_core, preferred_element_type=jnp.float32)
        fresh = (scaling * (sources[0, 0, moment].astype(jnp.float32) - far - near)).astype(
            jnp.bfloat16
        )
        outputs.append(fresh)
        squares = jnp.sum(jnp.square(fresh.astype(jnp.float32)), axis=0) / panel_total
        energy_rows.append(lax.psum(squares, ("row", "col")))
        if moment + 1 < step_count:
            gathered = lax.all_gather(fresh[None], "row", axis=0, tiled=True)
            column_past = jnp.concatenate([gathered[:, None], column_past[:, :-1]], axis=1)
            fresh_proj = jnp.einsum(
                "pta,ptx->pax", basis, gathered, preferred_element_type=jnp.float32
            ).astype(jnp.bfloat16)
            projected = jnp.concatenate([fresh_proj[:, None], projected[:, :-1]], axis=1)
    energies = jnp.stack(energy_rows, axis=0)
    new_steps = jnp.stack(outputs, axis=0)[None, None]
    return (new_steps, energies)


def solution(mesh):
    placed = (
        P("row", "col", None, None, None),
        P(None, "col", None, None, None),
        P("row", "col", None),
        P("row", None, None, None, "col", None, None),
        P("row", "col", None, None),
        P(None, "col", None, None),
        P("row", "col", None, None, None, None),
        P("row", "col", None),
        P("row", "col"),
    )
    return jax.shard_map(
        local,
        mesh=mesh,
        in_specs=placed,
        out_specs=(P("row", "col", None, None, None), P()),
        check_vma=False,
    )
```

profile of v0, /device:TPU:0, one launch (start us, length us, event | category | flops | bytes accessed | tf_op | source)
XLA Modules:
  0.0 396.4 jit_solution(5392760271177488294)
XLA Ops:
  7.2 3.5 reshape.69
  10.8 3.2 convolution_convert_fusion
  14.4 0.8 copy.20
  15.2 2.6 copy.29
  17.9 14.3 %while.40 = (s32[]{:T(128)}, f32[256,256]{1,0:T(8,128)S(1)}, s32[]{:T(128)}, bf16[3,256,8,256]{3,1,2,0:T(8,128)(2,1)S(1)}, s32[3]{0:T(128)S(1)}, /*index=5*/bf16...) while((s32[]{:T(128)}, f32[256,256]{1,0:T(8,128)S(1)}, s32[]{:T(128)}, ...), condition=%wide.region_2.3_spmd, body=%wide.region_1.2_spmd.sunk | while | flops 268500992 | bytes 2621629 | solution.py:55
  20.7 1.7 fusion.89
  25.3 1.7 fusion.89
  29.9 1.7 fusion.89
  32.2 4.3 %slice.41 = bf16[4,7,256,256]{3,2,1,0:T(8,128)(2,1)} slice(bf16[4,8,256,256]{3,2,1,0:T(8,128)(2,1)} %get-tuple-element.477), slice={[0:4], [0:7], [0:256], [0:256]} | slice | bytes 7340032 | tf_op jit(solution)/shard_map/slice | solution.py:70
  36.5 1.9 slice.40
  38.4 41.5 %reduce-scatter.13.cloned.1.call-done = bf16[32,256]{1,0:T(8,128)(2,1)} async-done(((bf16[256,256]{1,0:T(8,128)(2,1)}), bf16[32,256]{1,0:T(8,128)(2,1)}) %reduce-scatter.13.cloned.1.call-update) | async-done | bytes 16400
  79.9 1.7 multiply_reduce_fusion.3
  81.6 0.6 copy-done.6
  82.3 7.1 %all-gather = bf16[1024,256]{1,0:T(8,128)(2,1)S(1)} all-gather(bf16[256,256]{1,0:T(8,128)(2,1)S(1)} %get-tuple-element.197), channel_id=2, replica_groups=mesh['row'=4,'col'=8] {'row'}, dimensions={0}, use_global_device_ids=true | all-gather | bytes 655360 | tf_op jit(solution)/shard_map/all_gather | solution.py:69
  89.4 4.5 %pad_maximum_fusion = bf16[4,8,256,256]{3,2,1,0:T(8,128)(2,1)} fusion(bf16[4,1,256,256]{3,2,1,0:T(8,128)(2,1)S(1)} %bitcast.237, bf16[4,7,256,256]{3,2,1,0:T(8,128)(2,1)} %slice.41), kind=kLoop, calls=%fused_computation.29 | loop fusion | flops 2097152 | bytes 8388608 | tf_op jit(solution)/shard_map/concatenate | solution.py:70
  94.0 15.9 %while.41 = (s32[]{:T(128)}, f32[256,256]{1,0:T(8,128)S(1)}, s32[]{:T(128)}, bf16[3,256,8,256]{3,1,2,0:T(8,128)(2,1)S(1)}, s32[3]{0:T(128)S(1)}, /*index=5*/bf16...) while((s32[]{:T(128)}, f32[256,256]{1,0:T(8,128)S(1)}, s32[]{:T(128)}, ...), condition=%wide.region_5.6_spmd, body=%wide.region_4.5_spmd.sunk | while | flops 268500992 | bytes 2621629 | solution.py:55
  94.6 0.7 dynamic_slice.87
  97.4 1.7 fusion.92
  99.7 0.7 dynamic_slice.87
  102.5 1.7 fusion.92
  104.8 0.7 dynamic_slice.87
  107.6 1.7 fusion.92
  110.4 1.2 fusion.46
  111.6 1.1 pad_maximum_fusion.3
  112.7 2.0 fusion.43
  114.8 1.7 copy.22
  116.5 1.2 broadcast_multiply_fusion.3
  117.7 1.8 fusion.50
  119.5 3.5 fusion.25
  123.0 53.8 %reduce-scatter.15.cloned.1.call-done = bf16[32,256]{1,0:T(8,128)(2,1)} async-done(((bf16[256,256]{1,0:T(8,128)(2,1)}), bf16[32,256]{1,0:T(8,128)(2,1)}) %reduce-scatter.15.cloned.1.call-update) | async-done | bytes 16400
  176.8 1.7 multiply_reduce_fusion.2
  178.5 0.6 copy-done.7
  179.2 7.1 %all-gather.1 = bf16[1024,256]{1,0:T(8,128)(2,1)S(1)} all-gather(bf16[256,256]{1,0:T(8,128)(2,1)S(1)} %get-tuple-element.195), channel_id=3, replica_groups=mesh['row'=4,'col'=8] {'row'}, dimensions={0}, use_global_device_ids=true | all-gather | bytes 655360 | tf_op jit(solution)/shard_map/all_gather | solution.py:69
  186.3 4.5 %pad_maximum_fusion.1 = bf16[4,8,256,256]{3,2,1,0:T(8,128)(2,1)} fusion(bf16[4,1,256,256]{3,2,1,0:T(8,128)(2,1)S(1)} %bitcast.240, bf16[4,7,256,256]{3,2,1,0:T(8,128)(2,1)} %fusion.25), kind=kLoop, calls=%fused_computation.31 | loop fusion | flops 2097152 | bytes 8388608 | tf_op jit(solution)/shard_map/concatenate | solution.py:70
  190.9 15.8 %while.42 = (s32[]{:T(128)}, f32[256,256]{1,0:T(8,128)S(1)}, s32[]{:T(128)}, bf16[3,256,8,256]{3,1,2,0:T(8,128)(2,1)S(1)}, s32[3]{0:T(128)S(1)}, /*index=5*/bf16...) while((s32[]{:T(128)}, f32[256,256]{1,0:T(8,128)S(1)}, s32[]{:T(128)}, ...), condition=%wide.region_8.9_spmd, body=%wide.region_7.8_spmd.sunk | while | flops 268500992 | bytes 2621629 | solution.py:55
  191.5 0.7 dynamic_slice.90
  194.2 1.7 fusion.95
  196.6 0.7 dynamic_slice.90
  199.3 1.7 fusion.95
  201.6 0.7 dynamic_slice.90
  204.3 1.7 fusion.95
  206.6 1.2 fusion.47
  207.9 1.1 pad_maximum_fusion.4
  209.0 2.0 fusion.44
  211.0 1.7 copy.24
  212.7 1.2 broadcast_multiply_fusion.2
  214.0 1.8 fusion.49
  215.8 3.4 fusion.24
  219.2 53.8 %reduce-scatter.17.cloned.1.call-done = bf16[32,256]{1,0:T(8,128)(2,1)} async-done(((bf16[256,256]{1,0:T(8,128)(2,1)}), bf16[32,256]{1,0:T(8,128)(2,1)}) %reduce-scatter.17.cloned.1.call-update) | async-done | bytes 16400
  273.0 1.2 multiply_reduce_fusion.1
  274.2 7.1 %all-gather.2 = bf16[1024,256]{1,0:T(8,128)(2,1)S(1)} all-gather(bf16[256,256]{1,0:T(8,128)(2,1)S(1)} %get-tuple-element.193), channel_id=4, replica_groups=mesh['row'=4,'col'=8] {'row'}, dimensions={0}, use_global_device_ids=true | all-gather | bytes 655360 | tf_op jit(solution)/shard_map/all_gather | solution.py:69
  281.4 0.8 copy-done.5
  282.4 1.1 pad_maximum_fusion.5
  283.4 1.4 fusion.45
  284.8 0.8 copy.26
  285.6 4.5 %pad_maximum_fusion.2 = bf16[4,8,256,256]{3,2,1,0:T(8,128)(2,1)} fusion(bf16[4,7,256,256]{3,2,1,0:T(8,128)(2,1)} %fusion.24, bf16[4,1,256,256]{3,2,1,0:T(8,128)(2,1)} %bitcast.246), kind=kLoop, calls=%fused_computation.32 | loop fusion | flops 2097152 | bytes 8388608 | tf_op jit(solution)/shard_map/concatenate | solution.py:70
  290.1 15.3 %while.43 = (s32[]{:T(128)}, f32[256,256]{1,0:T(8,128)S(1)}, s32[]{:T(128)}, bf16[3,256,8,256]{3,1,2,0:T(8,128)(2,1)S(1)}, s32[3]{0:T(128)S(1)}, /*index=5*/bf16...) while((s32[]{:T(128)}, f32[256,256]{1,0:T(8,128)S(1)}, s32[]{:T(128)}, ...), condition=%wide.region_11.12_spmd, body=%wide.region_10.11_spmd.sunk | while | flops 268500992 | bytes 2621629 | solution.py:55
  293.3 1.7 fusion.98
  298.2 1.7 fusion.98
  303.1 1.7 fusion.98
  305.5 40.5 %reduce-scatter.19.cloned.1.call-done = bf16[32,256]{1,0:T(8,128)(2,1)} async-done(((bf16[256,256]{1,0:T(8,128)(2,1)}), bf16[32,256]{1,0:T(8,128)(2,1)}) %reduce-scatter.19.cloned.1.call-update) | async-done | bytes 16400
  346.0 1.2 multiply_reduce_fusion
  347.2 40.1 %all-reduce = (f32[1,256]{1,0:T(1,128)S(1)}, f32[1,256]{1,0:T(1,128)S(1)}, f32[1,256]{1,0:T(1,128)S(1)}, f32[1,256]{1,0:T(1,128)S(1)}) all-reduce(f32[1,256]{1,0:T(1,128)S(1)} %bitcast.261, f32[1,256]{1,0:T(1,128)S(1)} %bitcast.260, f32[1,256]{1,0:T(1,128)S(1)} %bitcast.259, ...), channel_id=1, replica_groups=mesh['row'=4,'col'=8] {'row','col'}, use_global_device_ids=true, to_apply=%region_19.20 | all-reduce | flops 1024 | bytes 8192 | tf_op jit(solution)/shard_map/psum | solution.py:67
  388.0 1.9 maximum_bitcast_fusion
  (58 shorter events, 5.5 us)
Async XLA Ops:
  7.2 3.6 copy-start
  7.2 72.7 %reduce-scatter.13.cloned.1.call-start = ((), (), s32[]{:S(2)}) async-start(), calls=%async_computation.4 | async-start | bytes 147456
  10.8 4.4 %copy-start.1 = (bf16[256,1024]{1,0:T(8,128)(2,1)}, bf16[256,1024]{1,0:T(8,128)(2,1)S(1)}, u32[]{:S(2)}) copy-start(bf16[256,1024]{1,0:T(8,128)(2,1)S(1)} %reshape.69) | copy-start | bytes 1572868
  14.0 1.2 copy-start.4
  14.0 3.9 copy-start.15
  15.2 161.6 %reduce-scatter.15.cloned.1.call-start = ((), (), s32[]{:S(2)}) async-start(), calls=%async_computation.5 | async-start | bytes 147456
  32.2 47.6 %copy-start.9 = (bf16[1,1,256,32]{2,3,1,0:T(8,128)(2,1)S(1)}, bf16[1,1,256,32]{2,3,1,0:T(8,128)(2,1)}, u32[]{:S(2)}) copy-start(bf16[1,1,256,32]{2,3,1,0:T(8,128)(2,1)} %param.21) | copy-start | bytes 49156
  32.2 47.6 %copy-start.10 = (f32[1,1,256]{2,1,0:T(1,128)S(1)}, f32[1,1,256]{2,1,0:T(1,128)}, u32[]{:S(2)}) copy-start(f32[1,1,256]{2,1,0:T(1,128)} %param.19) | copy-start | bytes 3076
  81.6 0.6 copy-start.6
  89.4 4.5 %copy-start.2 = (bf16[1024,256]{1,0:T(8,128)(2,1)}, bf16[1024,256]{1,0:T(8,128)(2,1)S(1)}, u32[]{:S(2)}) copy-start(bf16[1024,256]{1,0:T(8,128)(2,1)S(1)} %all-gather) | copy-start | bytes 1572868
  109.9 0.5 copy-start.16
  116.4 156.6 %reduce-scatter.17.cloned.1.call-start = ((), (), s32[]{:S(2)}) async-start(), calls=%async_computation.6 | async-start | bytes 147456
  119.5 57.3 %copy-start.11 = (f32[1,1,256]{2,1,0:T(1,128)S(1)}, f32[1,1,256]{2,1,0:T(1,128)}, u32[]{:S(2)}) copy-start(f32[1,1,256]{2,1,0:T(1,128)} %param.19) | copy-start | bytes 3076
  178.5 0.6 copy-start.7
  186.3 4.5 %copy-start.3 = (bf16[1024,256]{1,0:T(8,128)(2,1)}, bf16[1024,256]{1,0:T(8,128)(2,1)S(1)}, u32[]{:S(2)}) copy-start(bf16[1024,256]{1,0:T(8,128)(2,1)S(1)} %all-gather.1) | copy-start | bytes 1572868
  186.3 4.6 %copy-start.17 = (s32[3]{0:T(128)S(1)}, s32[3]{0:T(128)}, u32[]{:S(2)}) copy-start(s32[3]{0:T(128)} %copy-done.16) | copy-start | bytes 40
  212.7 133.3 %reduce-scatter.19.cloned.1.call-start = ((), (), s32[]{:S(2)}) async-start(), calls=%async_computation.7 | async-start | bytes 147456
  215.8 57.2 %copy-start.12 = (f32[1,1,256]{2,1,0:T(1,128)S(1)}, f32[1,1,256]{2,1,0:T(1,128)}, u32[]{:S(2)}) copy-start(f32[1,1,256]{2,1,0:T(1,128)} %param.19) | copy-start | bytes 3076
  274.2 7.2 %copy-start.8 = (bf16[256,256]{1,0:T(8,128)(2,1)}, bf16[256,256]{1,0:T(8,128)(2,1)S(1)}, u32[]{:S(2)}) copy-start(bf16[256,256]{1,0:T(8,128)(2,1)S(1)} %get-tuple-element.193) | copy-start | bytes 393220
  281.4 0.8 copy-start.5
  285.6 4.5 %copy-start.18 = (s32[3]{0:T(128)S(1)}, s32[3]{0:T(128)}, u32[]{:S(2)}) copy-start(s32[3]{0:T(128)} %copy-done.16) | copy-start | bytes 40
  290.1 57.1 %copy-start.13 = (f32[256]{0:T(256)S(1)}, f32[256]{0:T(256)}, u32[]{:S(2)}) copy-start(f32[256]{0:T(256)} %broadcast_multiply_fusion.3) | copy-start | bytes 3076
  290.1 57.1 %copy-start.14 = (f32[256]{0:T(256)S(1)}, f32[256]{0:T(256)}, u32[]{:S(2)}) copy-start(f32[256]{0:T(256)} %broadcast_multiply_fusion.2) | copy-start | bytes 3076
Sparse Core Ops, SparseCore 0:
  15.3 64.5 reduce-scatter.12
  116.6 60.1 reduce-scatter.14
  212.8 60.1 reduce-scatter.16
  285.7 60.2 reduce-scatter.18
where the time goes:
time: 398 us; the launch traced here: 396 us
  waiting for transfers between devices  190 us (48%)
  blocking collectives  61.5 us (15%)
  matrix products  37.7 us (9%)
  loops' own time  33.8 us (8%)
  other arithmetic  32.2 us (8%)
  local copies, waits for them, and re-layouts  27.2 us (7%)
  between operations  14 us (4%)
    unnamed x8, waiting for transfers between devices  190 us
    psum x1, blocking collectives, local(): energy_rows.append(lax.psum(squares, ('row', 'col')))  40.1 us
    another operation x4, loops' own time, local(): lax.fori_loop(0, live_count, add_block, jnp.zeros((tile_size, field_count...  33.8 us
    all_gather x3, blocking collectives, local(): gathered = lax.all_gather(fresh[None], 'row', axis=0, tiled=True)  21.4 us
    concatenate x5, other arithmetic, local(): jnp.concatenate([gathered[:, None], column_past[:, :-1]], axis=1)  20.4 us
    dot_general x12, matrix products, add_block(): return total + jnp.dot(block, source, preferred_element_type=jnp.float32)  20.1 us
    unnamed x43, local copies, waits for them, and re-layouts  10.1 us
  transfers between devices with their start and end apart: 4, of which 4 were waited for; matrix products, arithmetic and copies ran while one was open for 10% of the time, Pallas kernels for 0%

commit v1 on v0

--- a/solution.py
+++ b/solution.py
@@ -66,7 +66,16 @@
         squares = jnp.sum(jnp.square(fresh.astype(jnp.float32)), axis=0) / panel_total
         energy_rows.append(lax.psum(squares, ("row", "col")))
         if moment + 1 < step_count:
-            gathered = lax.all_gather(fresh[None], "row", axis=0, tiled=True)
+            ring = [fresh[None]]
+            for hop in range(3):
+                ring.append(
+                    lax.ppermute(ring[-1], "row", [(dev, (dev + 1) % 4) for dev in range(4)])
+                )
+            gathered = jnp.roll(
+                jnp.concatenate(ring[::-1], axis=0),
+                (lax.axis_index("row") + 1) * ring[0].shape[0],
+                axis=0,
+            )
             column_past = jnp.concatenate([gathered[:, None], column_past[:, :-1]], axis=1)
             fresh_proj = jnp.einsum(
                 "pta,ptx->pax", basis, gathered, preferred_element_type=jnp.float32

time: 398 us -> 372 us (0.935)
  blocking collectives: 61.5 us -> 40.1 us
  waiting for transfers between devices: 190 us -> 186 us
    unnamed x8, waiting for transfers between devices: 190 us -> 161 us
    ppermute x0 -> x9, waiting for transfers between devices: none -> 25 us  [local(): lax.ppermute(ring[-1], 'row', [(dev, (dev + 1) % 4) for dev in range(4)])]
    all_gather x3 -> x0, blocking collectives: 21.4 us -> none  [local(): gathered = lax.all_gather(fresh[None], 'row', axis=0, tiled=True)]
    concatenate x5, other arithmetic: 6.86 us -> 0.23 us  [local(): jnp.concatenate([fresh_proj[:, None], projected[:, :-1]], axis=1)]
    broadcast_in_dim x0 -> x3, other arithmetic: none -> 5.28 us  [local(): gathered[:, None]]
    dot_general x4, matrix products: 5.82 us -> 1.39 us  [local(): jnp.dot(core_matrix, projected.reshape(row_count * lag_count * rank_size,...]
    unnamed x43 -> x59, local copies, waits for them, and re-layouts: 10.1 us -> 7.08 us
  transfers between devices with their start and end apart: 4 -> 13, of which waited for: 4 -> 12; matrix products, arithmetic and copies ran while one was open for 10% -> 19% of each run, Pallas kernels for 0% -> 0%
where the time goes in v1:
time: 372 us; the launch traced here: 370 us
  waiting for transfers between devices  186 us (50%)
  blocking collectives  40.1 us (11%)
  matrix products  35.4 us (10%)
  loops' own time  33.6 us (9%)
  other arithmetic  31.1 us (8%)
  local copies, waits for them, and re-layouts  27.9 us (8%)
  between operations  14.2 us (4%)
    unnamed x8, waiting for transfers between devices  161 us
    psum x1, blocking collectives, local(): energy_rows.append(lax.psum(squares, ('row', 'col')))  40.1 us
    another operation x4, loops' own time, local(): lax.fori_loop(0, live_count, add_block, jnp.zeros((tile_size, field_count...  33.6 us
    ppermute x9, waiting for transfers between devices, local(): lax.ppermute(ring[-1], 'row', [(dev, (dev + 1) % 4) for dev in range(4)])  25 us
    concatenate x5, other arithmetic, local(): jnp.concatenate([gathered[:, None], column_past[:, :-1]], axis=1)  20.6 us
    dot_general x12, matrix products, add_block(): return total + jnp.dot(block, source, preferred_element_type=jnp.float32)  20.1 us
    dynamic_slice x12, local copies, waits for them, and re-layouts, add_block(): tiles_here[slot]  11.2 us
  transfers between devices with their start and end apart: 13, of which 12 were waited for; matrix products, arithmetic and copies ran while one was open for 19% of the time, Pallas kernels for 0%

profile of v1, /device:TPU:0, one launch (start us, length us, event | category | flops | bytes accessed | tf_op | source)
XLA Modules:
  0.0 369.7 jit_solution(4966316577009945899)
XLA Ops:
  7.2 3.5 reshape.69
  10.8 3.2 convolution_convert_fusion
  14.4 0.8 copy.14
  15.2 2.6 copy.23
  17.9 15.2 %while.40 = (s32[]{:T(128)}, f32[256,256]{1,0:T(8,128)S(1)}, s32[]{:T(128)}, bf16[3,256,8,256]{3,1,2,0:T(8,128)(2,1)S(1)}, s32[3]{0:T(128)S(1)}, /*index=5*/bf16...) while((s32[]{:T(128)}, f32[256,256]{1,0:T(8,128)S(1)}, s32[]{:T(128)}, ...), condition=%wide.region_2.3_spmd, body=%wide.region_1.2_spmd.sunk | while | flops 268500992 | bytes 2621629 | solution.py:55
  21.1 1.7 fusion.116
  25.9 1.7 fusion.116
  30.8 1.7 fusion.116
  33.1 46.7 %reduce-scatter.13.cloned.1.call-done = bf16[32,256]{1,0:T(8,128)(2,1)} async-done(((bf16[256,256]{1,0:T(8,128)(2,1)}), bf16[32,256]{1,0:T(8,128)(2,1)}) %reduce-scatter.13.cloned.1.call-update) | async-done | bytes 16400
  79.8 1.7 multiply_reduce_fusion.3
  82.2 4.4 %collective-permute-done = bf16[1,256,256]{2,1,0:T(8,128)(2,1)S(1)} collective-permute-done((bf16[1,256,256]{2,1,0:T(8,128)(2,1)S(1)}, bf16[1,256,256]{2,1,0:T(8,128)(2,1)S(1)}, u32[]{:S(2)}, u32[]{:S(2)}) %collective-permute-start) | collective-permute-done | bytes 131104 | tf_op jit(solution)/shard_map/ppermute | solution.py:72
  86.6 4.5 %collective-permute-done.1 = bf16[1,256,256]{2,1,0:T(8,128)(2,1)} collective-permute-done((bf16[1,256,256]{2,1,0:T(8,128)(2,1)S(1)}, bf16[1,256,256]{2,1,0:T(8,128)(2,1)}, u32[]{:S(2)}, u32[]{:S(2)}) %collective-permute-start.1) | collective-permute-done | bytes 131104 | tf_op jit(solution)/shard_map/ppermute | solution.py:72
  91.1 4.2 %slice.41 = bf16[4,7,256,256]{3,2,1,0:T(8,128)(2,1)} slice(bf16[4,8,256,256]{3,2,1,0:T(8,128)(2,1)} %get-tuple-element.478), slice={[0:4], [0:7], [0:256], [0:256]} | slice | bytes 7340032 | tf_op jit(solution)/shard_map/slice | solution.py:79
  95.4 1.8 slice.40
  97.2 1.8 fusion.46
  99.4 0.8 copy.16
  100.3 1.8 fusion.98
  102.0 4.6 %pad_maximum_fusion = bf16[4,8,256,256]{3,2,1,0:T(8,128)(2,1)} fusion(bf16[4,1,256,256]{3,2,1,0:T(8,128)(2,1)S(1)} %fusion.98, bf16[4,7,256,256]{3,2,1,0:T(8,128)(2,1)} %slice.41), kind=kLoop, calls=%fused_computation.29 | loop fusion | flops 2097152 | bytes 8388608 | tf_op jit(solution)/shard_map/concatenate | solution.py:79
  106.7 17.1 %while.41 = (s32[]{:T(128)}, f32[256,256]{1,0:T(8,128)S(1)}, s32[]{:T(128)}, bf16[3,256,8,256]{3,1,2,0:T(8,128)(2,1)S(1)}, s32[3]{0:T(128)}, /*index=5*/bf16[4,8...) while((s32[]{:T(128)}, f32[256,256]{1,0:T(8,128)S(1)}, s32[]{:T(128)}, ...), condition=%wide.region_5.7_spmd, body=%wide.region_4.6_spmd.sunk | while | flops 268500992 | bytes 2621629 | solution.py:55
  107.3 1.3 dynamic_slice.347
  110.5 1.7 fusion.119
  112.8 1.3 dynamic_slice.347
  115.9 1.7 fusion.119
  118.3 1.3 dynamic_slice.347
  121.4 1.7 fusion.119
  123.7 37.8 %reduce-scatter.15.cloned.1.call-done = bf16[32,256]{1,0:T(8,128)(2,1)} async-done(((bf16[256,256]{1,0:T(8,128)(2,1)}), bf16[32,256]{1,0:T(8,128)(2,1)}) %reduce-scatter.15.cloned.1.call-update) | async-done | bytes 16400
  161.6 2.4 multiply_reduce_fusion.2
  164.0 4.6 %collective-permute-done.3 = bf16[1,256,256]{2,1,0:T(8,128)(2,1)S(1)} collective-permute-done((bf16[1,256,256]{2,1,0:T(8,128)(2,1)}, bf16[1,256,256]{2,1,0:T(8,128)(2,1)S(1)}, u32[]{:S(2)}, u32[]{:S(2)}) %collective-permute-start.3) | collective-permute-done | bytes 131104 | tf_op jit(solution)/shard_map/ppermute | solution.py:72
  168.6 1.3 broadcast_multiply_fusion.3
  169.8 3.1 collective-permute-done.4
  173.0 3.5 fusion.25
  176.5 0.8 collective-permute-done.5
  177.4 1.7 fusion.47
  179.5 0.8 copy.18
  180.3 1.8 fusion.97
  182.1 4.6 %pad_maximum_fusion.1 = bf16[4,8,256,256]{3,2,1,0:T(8,128)(2,1)} fusion(bf16[4,1,256,256]{3,2,1,0:T(8,128)(2,1)S(1)} %fusion.97, bf16[4,7,256,256]{3,2,1,0:T(8,128)(2,1)} %fusion.25), kind=kLoop, calls=%fused_computation.31 | loop fusion | flops 2097152 | bytes 8388608 | tf_op jit(solution)/shard_map/concatenate | solution.py:79
  186.8 17.3 %while.42 = (s32[]{:T(128)}, f32[256,256]{1,0:T(8,128)S(1)}, s32[]{:T(128)}, bf16[3,256,8,256]{3,1,2,0:T(8,128)(2,1)S(1)}, s32[3]{0:T(128)}, /*index=5*/bf16[4,8...) while((s32[]{:T(128)}, f32[256,256]{1,0:T(8,128)S(1)}, s32[]{:T(128)}, ...), condition=%wide.region_8.10_spmd, body=%wide.region_7.9_spmd.sunk | while | flops 268500992 | bytes 2621629 | solution.py:55
  187.5 1.2 dynamic_slice.350
  190.6 1.7 fusion.122
  193.0 1.2 dynamic_slice.350
  196.2 1.7 fusion.122
  198.5 1.2 dynamic_slice.350
  201.7 1.7 fusion.122
  204.1 37.2 %reduce-scatter.17.cloned.1.call-done = bf16[32,256]{1,0:T(8,128)(2,1)} async-done(((bf16[256,256]{1,0:T(8,128)(2,1)}), bf16[32,256]{1,0:T(8,128)(2,1)}) %reduce-scatter.17.cloned.1.call-update) | async-done | bytes 16400
  241.3 1.2 multiply_reduce_fusion.1
  242.6 1.2 broadcast_multiply_fusion.2
  243.8 3.2 collective-permute-done.6
  247.0 3.4 fusion.24
  250.4 0.9 collective-permute-done.7
  251.4 0.9 collective-permute-start.8
  252.3 3.5 collective-permute-done.8
  255.8 0.7 copy-done.20
  256.4 0.7 fusion.48
  257.5 0.8 copy.20
  258.3 1.8 fusion.96
  260.1 4.4 %pad_maximum_fusion.2 = bf16[4,8,256,256]{3,2,1,0:T(8,128)(2,1)} fusion(bf16[4,7,256,256]{3,2,1,0:T(8,128)(2,1)} %fusion.24, bf16[4,1,256,256]{3,2,1,0:T(8,128)(2,1)S(1)} %fusion.96), kind=kLoop, calls=%fused_computation.32 | loop fusion | flops 2097152 | bytes 8388608 | tf_op jit(solution)/shard_map/concatenate | solution.py:79
  264.6 15.3 %while.43 = (s32[]{:T(128)}, f32[256,256]{1,0:T(8,128)S(1)}, s32[]{:T(128)}, bf16[3,256,8,256]{3,1,2,0:T(8,128)(2,1)S(1)}, s32[3]{0:T(128)S(1)}, /*index=5*/bf16...) while((s32[]{:T(128)}, f32[256,256]{1,0:T(8,128)S(1)}, s32[]{:T(128)}, ...), condition=%wide.region_11.13_spmd, body=%wide.region_10.12_spmd.sunk | while | flops 268500992 | bytes 2621629 | solution.py:55
  267.8 1.7 fusion.125
  272.7 1.7 fusion.125
  277.6 1.7 fusion.125
  279.9 39.4 %reduce-scatter.19.cloned.1.call-done = bf16[32,256]{1,0:T(8,128)(2,1)} async-done(((bf16[256,256]{1,0:T(8,128)(2,1)}), bf16[32,256]{1,0:T(8,128)(2,1)}) %reduce-scatter.19.cloned.1.call-update) | async-done | bytes 16400
  319.3 1.2 multiply_reduce_fusion
  320.5 1.9 maximum_bitcast_fusion
  322.4 40.1 %all-reduce = (f32[1,256]{1,0:T(1,128)S(1)}, f32[1,256]{1,0:T(1,128)S(1)}, f32[1,256]{1,0:T(1,128)S(1)}, f32[1,256]{1,0:T(1,128)S(1)}) all-reduce(f32[1,256]{1,0:T(1,128)S(1)} %bitcast.252, f32[1,256]{1,0:T(1,128)S(1)} %bitcast.251, f32[1,256]{1,0:T(1,128)S(1)} %bitcast.250, ...), channel_id=1, replica_groups=mesh['row'=4,'col'=8] {'row','col'}, use_global_device_ids=true, to_apply=%region_19.21 | all-reduce | flops 1024 | bytes 8192 | tf_op jit(solution)/shard_map/psum | solution.py:67
  (92 shorter events, 7.1 us)
Async XLA Ops:
  7.2 3.6 copy-start
  7.2 72.6 %reduce-scatter.13.cloned.1.call-start = ((), (), s32[]{:S(2)}) async-start(), calls=%async_computation.4 | async-start | bytes 147456
  10.8 4.3 %copy-start.1 = (bf16[256,1024]{1,0:T(8,128)(2,1)}, bf16[256,1024]{1,0:T(8,128)(2,1)S(1)}, u32[]{:S(2)}) copy-start(bf16[256,1024]{1,0:T(8,128)(2,1)S(1)} %reshape.69) | copy-start | bytes 1572868
  14.0 1.2 copy-start.5
  14.0 3.9 %copy-start.25 = (s32[1,1,3]{2,1,0:T(1,128)S(1)}, s32[1,1,3]{2,1,0:T(1,128)}, u32[]{:S(2)}) copy-start(s32[1,1,3]{2,1,0:T(1,128)} %param.26) | copy-start | bytes 40
  15.2 146.4 %reduce-scatter.15.cloned.1.call-start = ((), (), s32[]{:S(2)}) async-start(), calls=%async_computation.5 | async-start | bytes 147456
  17.9 62.0 %copy-start.15 = (bf16[1,1,256,32]{2,3,1,0:T(8,128)(2,1)S(1)}, bf16[1,1,256,32]{2,3,1,0:T(8,128)(2,1)}, u32[]{:S(2)}) copy-start(bf16[1,1,256,32]{2,3,1,0:T(8,128)(2,1)} %param.23) | copy-start | bytes 49156
  17.9 62.0 %copy-start.21 = (f32[1,1,256]{2,1,0:T(1,128)S(1)}, f32[1,1,256]{2,1,0:T(1,128)}, u32[]{:S(2)}) copy-start(f32[1,1,256]{2,1,0:T(1,128)} %param.21) | copy-start | bytes 3076
  81.6 0.7 copy-start.12
  82.2 4.4 %collective-permute-start = (bf16[1,256,256]{2,1,0:T(8,128)(2,1)S(1)}, bf16[1,256,256]{2,1,0:T(8,128)(2,1)S(1)}, u32[]{:S(2)}, u32[]{:S(2)}) collective-permute-start(bf16[1,256,256]{2,1,0:T(8,128)(2,1)S(1)} %bitcast.236), channel_id=1, source_target_pairs={{0,8},{8,16},{16,24},{24,0},{1,9},{9,17},{17,25},{25,1},{2,10},{10... | collective-permute-start | bytes 393224 | tf_op jit(solution)/shard_map/ppermute | solution.py:72
  82.2 15.0 %copy-start.13 = (bf16[256,256]{1,0:T(8,128)(2,1)S(1)}, bf16[256,256]{1,0:T(8,128)(2,1)}, u32[]{:S(2)}) copy-start(bf16[256,256]{1,0:T(8,128)(2,1)} %copy-done.12) | copy-start | bytes 393220
  86.6 12.4 %copy-start.16 = (bf16[1,256,256]{2,1,0:T(8,128)(2,1)}, bf16[1,256,256]{2,1,0:T(8,128)(2,1)S(1)}, u32[]{:S(2)}) copy-start(bf16[1,256,256]{2,1,0:T(8,128)(2,1)S(1)} %collective-permute-done) | copy-start | bytes 393220
  86.6 4.5 %collective-permute-start.1 = (bf16[1,256,256]{2,1,0:T(8,128)(2,1)S(1)}, bf16[1,256,256]{2,1,0:T(8,128)(2,1)}, u32[]{:S(2)}, u32[]{:S(2)}) collective-permute-start(bf16[1,256,256]{2,1,0:T(8,128)(2,1)S(1)} %collective-permute-done), channel_id=1, source_target_pairs={{0,8},{8,16},{16,24},{24,0},{1,9},{9,17},{17,25},{25,1},{2,10},{10... | collective-permute-start | bytes 393224 | tf_op jit(solution)/shard_map/ppermute | solution.py:72
  91.1 6.1 %collective-permute-start.2 = (bf16[1,256,256]{2,1,0:T(8,128)(2,1)}, bf16[1,256,256]{2,1,0:T(8,128)(2,1)}, u32[]{:S(2)}, u32[]{:S(2)}) collective-permute-start(bf16[1,256,256]{2,1,0:T(8,128)(2,1)} %collective-permute-done.1), channel_id=1, source_target_pairs={{0,8},{8,16},{16,24},{24,0},{1,9},{9,17},{17,25},{25,1},{2,10},{10... | collective-permute-start | bytes 393224 | tf_op jit(solution)/shard_map/ppermute | solution.py:72
  97.2 1.8 copy-start.8
  97.2 1.9 copy-start.2
  100.2 141.1 %reduce-scatter.17.cloned.1.call-start = ((), (), s32[]{:S(2)}) async-start(), calls=%async_computation.6 | async-start | bytes 147456
  102.0 4.6 %copy-start.6 = (bf16[4,1,256,256]{3,2,1,0:T(8,128)(2,1)}, bf16[4,1,256,256]{3,2,1,0:T(8,128)(2,1)S(1)}, u32[]{:S(2)}) copy-start(bf16[4,1,256,256]{3,2,1,0:T(8,128)(2,1)S(1)} %fusion.98) | copy-start | bytes 1572868
  164.0 4.6 %collective-permute-start.3 = (bf16[1,256,256]{2,1,0:T(8,128)(2,1)}, bf16[1,256,256]{2,1,0:T(8,128)(2,1)S(1)}, u32[]{:S(2)}, u32[]{:S(2)}) collective-permute-start(bf16[1,256,256]{2,1,0:T(8,128)(2,1)} %bitcast.38), channel_id=1, source_target_pairs={{0,8},{8,16},{16,24},{24,0},{1,9},{9,17},{17,25},{25,1},{2,10},{10... | collective-permute-start | bytes 393224 | tf_op jit(solution)/shard_map/ppermute | solution.py:72
  164.0 12.5 %copy-start.9 = (bf16[4,7,32,256]{3,2,1,0:T(8,128)(2,1)S(1)}, bf16[4,7,32,256]{3,2,1,0:T(8,128)(2,1)}, u32[]{:S(2)}) copy-start(bf16[4,7,32,256]{3,2,1,0:T(8,128)(2,1)} %slice.40) | copy-start | bytes 1376260
  168.6 4.4 %collective-permute-start.4 = (bf16[1,256,256]{2,1,0:T(8,128)(2,1)S(1)}, bf16[1,256,256]{2,1,0:T(8,128)(2,1)S(1)}, u32[]{:S(2)}, u32[]{:S(2)}) collective-permute-start(bf16[1,256,256]{2,1,0:T(8,128)(2,1)S(1)} %collective-permute-done.3), channel_id=1, source_target_pairs={{0,8},{8,16},{16,24},{24,0},{1,9},{9,17},{17,25},{25,1},{2,10},{10... | collective-permute-start | bytes 393224 | tf_op jit(solution)/shard_map/ppermute | solution.py:72
  173.0 4.4 %copy-start.18 = (bf16[1,256,256]{2,1,0:T(8,128)(2,1)}, bf16[1,256,256]{2,1,0:T(8,128)(2,1)S(1)}, u32[]{:S(2)}) copy-start(bf16[1,256,256]{2,1,0:T(8,128)(2,1)S(1)} %collective-permute-done.4) | copy-start | bytes 393220
  173.0 4.4 %collective-permute-start.5 = (bf16[1,256,256]{2,1,0:T(8,128)(2,1)S(1)}, bf16[1,256,256]{2,1,0:T(8,128)(2,1)S(1)}, u32[]{:S(2)}, u32[]{:S(2)}) collective-permute-start(bf16[1,256,256]{2,1,0:T(8,128)(2,1)S(1)} %collective-permute-done.4), channel_id=1, source_target_pairs={{0,8},{8,16},{16,24},{24,0},{1,9},{9,17},{17,25},{25,1},{2,10},{10... | collective-permute-start | bytes 393224 | tf_op jit(solution)/shard_map/ppermute | solution.py:72
  176.5 2.7 copy-start.3
  176.5 2.5 copy-start.10
  177.4 1.8 copy-start.19
  180.3 139.0 %reduce-scatter.19.cloned.1.call-start = ((), (), s32[]{:S(2)}) async-start(), calls=%async_computation.7 | async-start | bytes 147456
  182.1 4.7 %copy-start.7 = (bf16[4,1,256,256]{3,2,1,0:T(8,128)(2,1)}, bf16[4,1,256,256]{3,2,1,0:T(8,128)(2,1)S(1)}, u32[]{:S(2)}) copy-start(bf16[4,1,256,256]{3,2,1,0:T(8,128)(2,1)S(1)} %fusion.97) | copy-start | bytes 1572868
  241.3 9.1 %copy-start.11 = (bf16[4,7,32,256]{3,2,1,0:T(8,128)(2,1)S(1)}, bf16[4,7,32,256]{3,2,1,0:T(8,128)(2,1)}, u32[]{:S(2)}) copy-start(bf16[4,7,32,256]{3,2,1,0:T(8,128)(2,1)} %copy-done.10) | copy-start | bytes 1376260
  242.5 13.2 %copy-start.14 = (bf16[256,256]{1,0:T(8,128)(2,1)}, bf16[256,256]{1,0:T(8,128)(2,1)S(1)}, u32[]{:S(2)}) copy-start(bf16[256,256]{1,0:T(8,128)(2,1)S(1)} %get-tuple-element.194) | copy-start | bytes 393220
  242.5 4.4 %collective-permute-start.6 = (bf16[1,256,256]{2,1,0:T(8,128)(2,1)S(1)}, bf16[1,256,256]{2,1,0:T(8,128)(2,1)S(1)}, u32[]{:S(2)}, u32[]{:S(2)}) collective-permute-start(bf16[1,256,256]{2,1,0:T(8,128)(2,1)S(1)} %bitcast.240), channel_id=1, source_target_pairs={{0,8},{8,16},{16,24},{24,0},{1,9},{9,17},{17,25},{25,1},{2,10},{10... | collective-permute-start | bytes 393224 | tf_op jit(solution)/shard_map/ppermute | solution.py:72
  247.0 4.4 %collective-permute-start.7 = (bf16[1,256,256]{2,1,0:T(8,128)(2,1)S(1)}, bf16[1,256,256]{2,1,0:T(8,128)(2,1)S(1)}, u32[]{:S(2)}, u32[]{:S(2)}) collective-permute-start(bf16[1,256,256]{2,1,0:T(8,128)(2,1)S(1)} %collective-permute-done.6), channel_id=1, source_target_pairs={{0,8},{8,16},{16,24},{24,0},{1,9},{9,17},{17,25},{25,1},{2,10},{10... | collective-permute-start | bytes 393224 | tf_op jit(solution)/shard_map/ppermute | solution.py:72
  250.4 6.8 %copy-start.4 = (bf16[256,1024]{1,0:T(8,128)(2,1)S(1)}, bf16[256,1024]{1,0:T(8,128)(2,1)}, u32[]{:S(2)}) copy-start(bf16[256,1024]{1,0:T(8,128)(2,1)} %copy-done.1) | copy-start | bytes 1572868
  251.4 5.8 %copy-start.17 = (bf16[1,256,256]{2,1,0:T(8,128)(2,1)}, bf16[1,256,256]{2,1,0:T(8,128)(2,1)S(1)}, u32[]{:S(2)}) copy-start(bf16[1,256,256]{2,1,0:T(8,128)(2,1)S(1)} %collective-permute-done.7) | copy-start | bytes 393220
  251.4 4.4 %collective-permute-start.8 = (bf16[1,256,256]{2,1,0:T(8,128)(2,1)S(1)}, bf16[1,256,256]{2,1,0:T(8,128)(2,1)S(1)}, u32[]{:S(2)}, u32[]{:S(2)}) collective-permute-start(bf16[1,256,256]{2,1,0:T(8,128)(2,1)S(1)} %collective-permute-done.7), channel_id=1, source_target_pairs={{0,8},{8,16},{16,24},{24,0},{1,9},{9,17},{17,25},{25,1},{2,10},{10... | collective-permute-start | bytes 393224 | tf_op jit(solution)/shard_map/ppermute | solution.py:72
  255.8 0.7 copy-start.20
  260.1 4.5 %copy-start.26 = (s32[3]{0:T(128)S(1)}, s32[3]{0:T(128)}, u32[]{:S(2)}) copy-start(s32[3]{0:T(128)} %get-tuple-element.507) | copy-start | bytes 40
  264.6 54.8 %copy-start.22 = (f32[1,1,256]{2,1,0:T(1,128)S(1)}, f32[1,1,256]{2,1,0:T(1,128)}, u32[]{:S(2)}) copy-start(f32[1,1,256]{2,1,0:T(1,128)} %param.21) | copy-start | bytes 3076
  264.6 57.8 %copy-start.23 = (f32[256]{0:T(256)S(1)}, f32[256]{0:T(256)}, u32[]{:S(2)}) copy-start(f32[256]{0:T(256)} %broadcast_multiply_fusion.3) | copy-start | bytes 3076
  264.6 57.8 %copy-start.24 = (f32[256]{0:T(256)S(1)}, f32[256]{0:T(256)}, u32[]{:S(2)}) copy-start(f32[256]{0:T(256)} %broadcast_multiply_fusion.2) | copy-start | bytes 3076
Sparse Core Ops, SparseCore 0:
  15.3 64.5 reduce-scatter.12
  100.3 61.1 reduce-scatter.14
  180.4 60.8 reduce-scatter.16
  258.4 60.8 reduce-scatter.18
